TPU v7x, 32 devices: a whole 2x2x4 slice. The times are simulated.
32 devices in a mesh: row: 4 (over z), col: 2 (over y), layer: 4 (over x, core).
Axes of the slice: x: 2, y: 2, z: 4, core: 2. Of those that a mesh axis runs over, the one named last changes fastest.
Arguments:
- amplitudes: float32 [2016, 73536], P('row', ('layer', 'col')), may hold values from -6 to 6
- integrals: float32 [73536, 768], P(('layer', 'col'), 'row'), may hold values from -0.03125 to 0.03125
- occ_energy: float32 [64], replicated, may hold values from -2 to -0.5
- vir_energy: float32 [384], replicated, may hold values from 0.2 to 3
Outputs:
- ladder: float32 [2016, 768], P('col', ('row', 'layer'))
- amplitude_step: float32 [2016, 768], P('col', ('row', 'layer'))
All inputs are finite; a program needn't handle non-finite values.
Results may differ from a plain program's by a relative error of at most 0.00007.
Values sent between devices are 32-bit elements; how exact they have to be, the bound alone decides.
A program may use at most 128 MiB of HBM per device.

v0:
```python
import jax
import jax.numpy as jnp
import numpy as np
from jax import lax
from jax.sharding import PartitionSpec as P


def lookup(indices, values_table):
    positions = jnp.arange(values_table.shape[0], dtype=jnp.int32)
    picked = jnp.where(indices[:, None] == positions[None, :], values_table[None, :], 0.0)
    return jnp.sum(picked, axis=1)


def owner_blocks(partial_sum):
    col_count = lax.axis_size("col")
    layer_count = lax.axis_size("layer")
    pair_rows = partial_sum.shape[0] // col_count
    slab_cols = partial_sum.shape[1] // layer_count
    blocks = partial_sum.reshape(col_count, pair_rows, layer_count, slab_cols)
    return blocks.transpose(0, 2, 1, 3).reshape(col_count * layer_count * pair_rows, slab_cols)


def shards(amplitudes, integrals, occ_energy, vir_energy):
    partial_rows = jnp.dot(
        amplitudes,
        lax.all_gather(integrals, "row", axis=1, tiled=True),
        precision=lax.Precision.HIGHEST,
        preferred_element_type=jnp.float32,
    )
    partial_sum = lax.all_to_all(partial_rows, "row", split_axis=1, concat_axis=0, tiled=True)
    ladder = lax.psum_scatter(
        owner_blocks(partial_sum), ("col", "layer"), scatter_dimension=0, tiled=True
    )
    pair_rows = ladder.shape[0]
    slab_cols = ladder.shape[1]
    occupied = occ_energy.shape[0]
    virtuals = vir_energy.shape[0]
    first_np, second_np = np.triu_indices(occupied, 1)
    ij_start = lax.axis_index("col") * pair_rows
    ab_start = (
        lax.axis_index("row") * lax.axis_size("layer") + lax.axis_index("layer")
    ) * slab_cols
    first_index = lax.dynamic_slice_in_dim(
        jnp.asarray(first_np, dtype=jnp.int32), ij_start, pair_rows
    )
    second_index = lax.dynamic_slice_in_dim(
        jnp.asarray(second_np, dtype=jnp.int32), ij_start, pair_rows
    )
    pair_sum = lookup(first_index, occ_energy) + lookup(second_index, occ_energy)
    ab_index = ab_start + jnp.arange(slab_cols, dtype=jnp.int32)
    vir_sum = lookup(ab_index // virtuals, vir_energy) + lookup(ab_index % virtuals, vir_energy)
    denominator = pair_sum[:, None] - vir_sum[None, :]
    return (ladder, ladder / denominator)


def solution(mesh):
    in_specs = (P("row", ("layer", "col")), P(("layer", "col"), "row"), P(), P())
    out_specs = (P("col", ("row", "layer")), P("col", ("row", "layer")))
    return jax.shard_map(shards, mesh=mesh, in_specs=in_specs, out_specs=out_specs, check_vma=False)
```

profile of v0, /device:TPU:17, one launch (start us, length us, event | category | flops | bytes accessed | tf_op | source)
XLA Modules:
  0.0 640.2 jit_solution(13388910612487923109)
XLA Ops:
  7.2 0.0 all-gather.2.cloned.1.call-start
  7.2 0.7 all-gather.2.cloned.1.call-update
  7.9 0.0 reduce-scatter.4.cloned.1.call-start
  7.9 476.9 %all-gather.2.cloned.1.call-done = f32[9192,768]{0,1:T(8,128)} async-done(((f32[9192,192]{0,1:T(8,128)}), f32[9192,768]{0,1:T(8,128)}) %all-gather.2.cloned.1.call-update) | async-done | bytes 28237840 | tf_op jit(solution)/shard_map/all_gather | solution.py:26
  484.8 48.5 %fusion.1 = f32[504,768]{0,1:T(8,128)S(1)} fusion(f32[504,9192]{1,0:T(8,128)} %param.6, f32[9192,768]{0,1:T(8,128)} %all-gather.2.cloned.1.call-done), kind=kOutput, calls=%fused_computation.13 | convolution fusion | flops 42695589888 | bytes 48317184 | tf_op jit(solution)/shard_map/dot_general | solution.py:24
  533.3 0.0 copy-start.2
  533.3 0.0 copy-start.1
  533.4 0.0 copy-start.3
  533.4 0.0 copy-start.4
  533.4 39.0 %all_to_all.16 = f32[504,4,192]{0,2,1:T(8,128)S(1)} all-to-all(f32[504,4,192]{0,2,1:T(8,128)S(1)} %bitcast.12), channel_id=1, replica_groups=mesh['row'=4,'col'=2,'layer'=4] {'row'}, dimensions={1} | all-to-all | bytes 3096576 | tf_op jit(solution)/shard_map/all_to_all | solution.py:30
  572.4 1.0 copy.17
  573.4 1.9 reshape.46
  575.3 3.1 copy.22
  578.4 0.0 reduce-scatter.4.cloned.1.call-update
  578.4 0.0 copy-done.2
  578.4 0.1 dynamic_slice.7
  578.5 0.0 copy-done.1
  578.5 0.1 dynamic_slice.6
  578.6 0.0 copy-done.3
  578.6 0.2 select_reduce_fusion.2
  578.8 0.0 copy-done.4
  578.8 0.2 select_reduce_fusion
  579.0 52.3 %reduce-scatter.4.cloned.1.call-done = f32[1008,48]{1,0:T(8,128)} async-done(((f32[8064,48]{1,0:T(8,128)}), f32[1008,48]{1,0:T(8,128)}) %reduce-scatter.4.cloned.1.call-update) | async-done | bytes 193552
  631.3 1.2 copy.21
  632.5 0.0 copy-start
  632.5 0.8 subtract_divide_fusion
  633.3 0.0 copy-done
  (3 shorter events, 0.0 us)
Async XLA Ops:
  7.2 477.6 %all-gather.2.cloned.1.call-start = ((), (), s32[]{:S(2)}) async-start(), calls=%async_computation.2 | async-start | bytes 35389440 | tf_op jit(solution)/shard_map/all_gather | solution.py:26
  7.9 623.4 %reduce-scatter.4.cloned.1.call-start = ((), (), s32[]{:S(2)}) async-start(), calls=%async_computation.3 | async-start | bytes 4644864
  533.3 45.1 %copy-start.2 = (s32[2016]{0:T(1024)S(1)}, s32[2016]{0:T(1024)}, u32[]{:S(2)}) copy-start(s32[2016]{0:T(1024)} %constant.48.clone) | copy-start | bytes 24196
  533.3 45.2 %copy-start.1 = (s32[2016]{0:T(1024)S(1)}, s32[2016]{0:T(1024)}, u32[]{:S(2)}) copy-start(s32[2016]{0:T(1024)} %constant.47.clone) | copy-start | bytes 24196
  533.4 45.3 %copy-start.3 = (f32[384]{0:T(512)S(1)}, f32[384]{0:T(512)}, u32[]{:S(2)}) copy-start(f32[384]{0:T(512)} %param.9) | copy-start | bytes 4612
  533.4 45.5 %copy-start.4 = (f32[64]{0:T(128)S(1)}, f32[64]{0:T(128)}, u32[]{:S(2)}) copy-start(f32[64]{0:T(128)} %param.8) | copy-start | bytes 772
  632.5 0.8 copy-start
Sparse Core Ops, SparseCore 0:
  9.6 475.2 all-gather.1
  578.6 52.7 reduce-scatter.3
where the time goes:
time: 642 us; the launch traced here: 640 us
  waiting for transfers between devices  530 us (83%)
  matrix products  48.5 us (8%)
  blocking collectives  39 us (6%)
  between operations  14.2 us (2%)
  local copies, waits for them, and re-layouts  7.39 us (1%)
    all_gather x1, waiting for transfers between devices, shards(): lax.all_gather(integrals, 'row', axis=1, tiled=True)  477 us
    unnamed x3, waiting for transfers between devices  53 us
    dot_general x1, matrix products, shards(): jnp.dot(amplitudes, lax.all_gather(integrals, 'row', axis=1, tiled=True),...  48.5 us
    all_to_all x1, blocking collectives, shards(): lax.all_to_all(partial_rows, 'row', split_axis=1, concat_axis=0, tiled=True)  39 us
  transfers between devices with their start and end apart: 2, of which 2 were waited for; matrix products, arithmetic and copies ran while one was open for 0% of the time, Pallas kernels for 0%

commit v1 on v0

--- a/solution.py
+++ b/solution.py
@@ -20,7 +20,137 @@
     return blocks.transpose(0, 2, 1, 3).reshape(col_count * layer_count * pair_rows, slab_cols)
 
 
-def shards(amplitudes, integrals, occ_energy, vir_energy):
+def contract(columns, rows):
+    return lax.dot_general(
+        columns,
+        rows,
+        (((1,), (1,)), ((), ())),
+        precision=lax.Precision.HIGH,
+        preferred_element_type=jnp.float32,
+    )
+
+
+def near_depth(depth):
+    return -(-depth // (6 * 128)) * 128
+
+
+def settled(value):
+    return lax.optimization_barrier(value)
+
+
+def line_exchange(amplitudes, integrals):
+    row = lax.axis_index("row")
+    low = row < 2
+    edge = (row == 0) | (row == 3)
+    pair_rows = amplitudes.shape[0]
+    depth, width = integrals.shape
+    near = near_depth(depth)
+    far = 2 * near
+    columns = integrals.T
+    parts = [0, far + near]
+    firsts = [columns[:, start : start + far] for start in parts]
+    up_pairs = [(0, 1), (1, 2), (2, 3)]
+    down_pairs = [(3, 2), (2, 1), (1, 0)]
+
+    def shift(up_payload, down_payload):
+        return (
+            lax.ppermute(up_payload, "row", up_pairs),
+            lax.ppermute(down_payload, "row", down_pairs),
+        )
+
+    def sides(pair):
+        up, down = pair
+        return jnp.where(low, down, up), jnp.where(low, up, down)
+
+    def kept(value):
+        return jnp.where(edge, 0.0, value)
+
+    hop1 = [shift(first, first) for first in firsts]
+    seconds = []
+    shared = []
+    for start in parts:
+        end = min(start + far + near, depth)
+        pad = start + far + near - end
+        seconds.append(jnp.pad(columns[:, start + far : end], ((0, 0), (0, pad))))
+        shared.append(
+            jnp.pad(amplitudes[:, start + far : end], ((0, 3 * width - pair_rows), (0, pad)))
+        )
+    hop2 = []
+    for part in range(2):
+        up1, down1 = hop1[part]
+        edge2 = jnp.concatenate([seconds[part], shared[part][:width]], axis=1)
+        hop2.append(
+            shift(jnp.where(row == 0, edge2, up1), jnp.where(row == 3, edge2, down1))
+        )
+    hop3 = []
+    for part in range(2):
+        up2, down2 = hop2[part]
+        edge3 = jnp.concatenate(
+            [shared[part][width : 2 * width], shared[part][2 * width :]], axis=1
+        )
+        up_mid = jnp.concatenate([seconds[part], up2[:, :near]], axis=1)
+        down_mid = jnp.concatenate([seconds[part], down2[:, :near]], axis=1)
+        hop3.append(
+            shift(
+                jnp.where(row == 0, edge3, jnp.where(row == 1, up_mid, up2)),
+                jnp.where(row == 3, edge3, jnp.where(row == 2, down_mid, down2)),
+            )
+        )
+    own = settled(contract(columns, amplitudes))
+    slot1 = slot2 = slot3 = extra1 = extra2 = extra3 = 0.0
+    for part, start in enumerate(parts):
+        rows_first = amplitudes[:, start : start + far]
+        own_rows = shared[part][:pair_rows]
+        inner1, outer1 = sides(hop1[part])
+        slot1 += settled(contract(inner1, rows_first))
+        third = settled(contract(outer1, rows_first))
+        inner2, outer2 = sides(hop2[part])
+        slot2 += settled(contract(inner2, rows_first))
+        third = settled(third + contract(outer2[:, :near], own_rows))
+        inner3, outer3 = sides(hop3[part])
+        last = settled(contract(inner3, rows_first))
+        slot3 += jnp.where(edge, last, third)
+        columns3 = jnp.concatenate([inner3[:, :near], inner3[:, near:]], axis=0)
+        columns3 = kept(columns3)
+        mixed = settled(contract(columns3, own_rows))
+        slot1 += mixed[:width]
+        slot2 += mixed[width:]
+        sent = jnp.concatenate([outer2[:, near:], outer3[:, :near], outer3[:, near:]], axis=0)
+        sent = kept(sent[:pair_rows])
+        three = settled(contract(jnp.concatenate([seconds[part], columns3], axis=0), sent))
+        extra1 += three[:width]
+        extra2 += three[width : 2 * width]
+        extra3 += three[2 * width :]
+
+    slots = [own, slot1, slot2, slot3]
+    order = [jnp.where(edge, slots[at], slots[(at + 3) % 4]) for at in range(4)]
+    extra = [jnp.zeros_like(extra1), extra1, extra2, extra3]
+    both = [jnp.stack([order[at], extra[at]]) for at in range(4)]
+    both = [jnp.where(low, both[at], both[3 - at]) for at in range(4)]
+    layers = lax.axis_size("layer")
+    slab = width // layers
+    stacked = jnp.stack(both).reshape(2, 2, 2, layers, slab, pair_rows)
+    stacked = stacked.transpose(0, 3, 1, 2, 4, 5).reshape(-1, 2, 2, slab, pair_rows)
+    mine = lax.psum_scatter(stacked, ("col", "layer"), scatter_dimension=0, tiled=True)[0]
+    odd = row % 2 == 1
+    same = jnp.where(odd, mine[1], mine[0])
+    other = jnp.where(odd, mine[0], mine[1])
+    same_pairs = []
+    other_pairs = []
+    for source_row in range(4):
+        for source_col in range(2):
+            bit = source_row % 2
+            source = source_row * 2 + source_col
+            same_pairs.append((source, (2 * source_col + bit) * 2 + source_row // 2))
+            other_pairs.append((source, (2 * source_col + 1 - bit) * 2 + source_row // 2))
+    same = lax.ppermute(same, ("row", "col"), same_pairs)
+    other = lax.ppermute(other, ("row", "col"), other_pairs)
+    even_rows = jnp.where(odd, other, same)
+    odd_rows = jnp.where(odd, same, other)
+    return jnp.concatenate([even_rows[0] + odd_rows[1], odd_rows[0] + even_rows[1]], axis=1)
+
+
+def gathered(amplitudes, integrals):
     partial_rows = jnp.dot(
         amplitudes,
         lax.all_gather(integrals, "row", axis=1, tiled=True),
@@ -28,9 +158,19 @@
         preferred_element_type=jnp.float32,
     )
     partial_sum = lax.all_to_all(partial_rows, "row", split_axis=1, concat_axis=0, tiled=True)
-    ladder = lax.psum_scatter(
+    return lax.psum_scatter(
         owner_blocks(partial_sum), ("col", "layer"), scatter_dimension=0, tiled=True
     )
+
+
+def shards(amplitudes, integrals, occ_energy, vir_energy):
+    in_line = lax.axis_size("row") == 4 and lax.axis_size("col") == 2
+    fits = amplitudes.shape[0] <= 3 * integrals.shape[1]
+    depth = integrals.shape[0]
+    if in_line and fits and depth > 5 * near_depth(depth):
+        ladder = line_exchange(amplitudes, integrals).T
+    else:
+        ladder = gathered(amplitudes, integrals)
     pair_rows = ladder.shape[0]
     slab_cols = ladder.shape[1]
     occupied = occ_energy.shape[0]

time: 642 us -> 434 us (0.68)
  waiting for transfers between devices: 530 us -> 215 us
  local copies, waits for them, and re-layouts: 7.39 us -> 47.3 us
  starting transfers between devices: 0.08 us -> 39.7 us
  blocking collectives: 39 us -> 0 us
  other arithmetic: 1.14 us -> 38.1 us
  matrix products: 48.5 us -> 72.4 us
    all_gather x1 -> x0, waiting for transfers between devices: 477 us -> none  [shards(): lax.all_gather(integrals, 'row', axis=1, tiled=True)]
    ppermute x0 -> x14, waiting for transfers between devices: none -> 168 us  [the longest x6 134 us: shift(): lax.ppermute(up_payload, 'row', up_pairs)]
    unnamed x3 -> x1, waiting for transfers between devices: 53 us -> 0.02 us
    reduce_scatter x0 -> x1, waiting for transfers between devices: none -> 46.4 us  [line_exchange(): lax.psum_scatter(stacked, ('col', 'layer'), scatter_dimension=0, tiled=True)]
    ppermute x0 -> x14, starting transfers between devices: none -> 39.7 us  [the longest x6 18.7 us: shift(): lax.ppermute(down_payload, 'row', down_pairs)]
    all_to_all x1 -> x0, blocking collectives: 39 us -> none  [shards(): lax.all_to_all(partial_rows, 'row', split_axis=1, concat_axis=0, tiled=True)]
    slice x0 -> x19, local copies, waits for them, and re-layouts: none -> 34.3 us  [the longest x2 5.35 us: line_exchange(): shared[part][width:2 * width]]
    select_n x0 -> x11, other arithmetic: none -> 32.5 us  [the longest x2 16.6 us: line_exchange(): jnp.where(row == 0, edge3, jnp.where(row == 1, up_mid, up2))]
  transfers between devices with their start and end apart: 2 -> 15, of which waited for: 2 -> 15; matrix products, arithmetic and copies ran while one was open for 0% -> 29% of each run, Pallas kernels for 0% -> 0%
where the time goes in v1:
time: 434 us; the launch traced here: 427 us
  waiting for transfers between devices  215 us (50%)
  matrix products  72.4 us (17%)
  local copies, waits for them, and re-layouts  47.3 us (11%)
  starting transfers between devices  39.7 us (9%)
  other arithmetic  38.1 us (9%)
  between operations  15.2 us (4%)
    ppermute x6, waiting for transfers between devices, shift(): lax.ppermute(up_payload, 'row', up_pairs)  134 us
    dot_general x15, matrix products, contract(): lax.dot_general(columns, rows, (((1,), (1,)), ((), ())), precision=lax.Pr...  72.4 us
    reduce_scatter x1, waiting for transfers between devices, line_exchange(): lax.psum_scatter(stacked, ('col', 'layer'), scatter_dimension=0, tiled=True)  46.4 us
    ppermute x6, starting transfers between devices, shift(): lax.ppermute(down_payload, 'row', down_pairs)  18.7 us
    select_n x2, other arithmetic, line_exchange(): jnp.where(row == 0, edge3, jnp.where(row == 1, up_mid, up2))  16.6 us
    ppermute x6, waiting for transfers between devices, shift(): lax.ppermute(down_payload, 'row', down_pairs)  16.6 us
    ppermute x6, starting transfers between devices, shift(): lax.ppermute(up_payload, 'row', up_pairs)  15.8 us
    ppermute x1, waiting for transfers between devices, line_exchange(): same = lax.ppermute(same, ('row', 'col'), same_pairs)  9.5 us
  transfers between devices with their start and end apart: 15, of which 15 were waited for; matrix products, arithmetic and copies ran while one was open for 29% of the time, Pallas kernels for 0%

profile of v1, /device:TPU:17, one launch (start us, length us, event | category | flops | bytes accessed | tf_op | source)
XLA Modules:
  0.0 427.2 jit_solution(15875788218315381873)
XLA Ops:
  7.2 5.2 %fusion.83 = (f32[192,3072]{1,0:T(8,128)}, f32[192,3072]{1,0:T(8,128)}) fusion(f32[192,9192]{1,0:T(8,128)} %bitcast.46), kind=kLoop, calls=%fused_computation.141 | loop fusion | bytes 9437184 | tf_op jit(solution)/shard_map/slice | solution.py:51
  12.4 3.2 collective-permute-start.3
  17.7 4.6 %collective-permute-start.9 = (f32[192,3072]{1,0:T(8,128)}, f32[192,3072]{1,0:T(8,128)}, u32[]{:S(2)}, u32[]{:S(2)}) collective-permute-start(f32[192,3072]{1,0:T(8,128)} %get-tuple-element.17), channel_id=1, source_target_pairs={{0,8},{8,16},{16,24},{1,9},{9,17},{17,25},{2,10},{10,18},{18,26},{... | collective-permute-start | bytes 7077896 | tf_op jit(solution)/shard_map/ppermute | solution.py:57
  24.2 12.9 %fusion.90 = f32[192,504]{1,0:T(8,128)} fusion(f32[9192,192]{0,1:T(8,128)S(1)} %copy-done.2, f32[504,9192]{1,0:T(8,128)} %param.6), kind=kOutput, calls=%fused_computation.148 | convolution fusion | flops 5336948736 | bytes 25977600 | tf_op jit(solution)/shard_map/dot_general | solution.py:24
  41.9 3.7 slice.166
  50.7 3.6 fusion.82
  54.3 12.4 %collective-permute-done.3 = f32[192,3072]{1,0:T(8,128)} collective-permute-done((f32[192,3072]{1,0:T(8,128)}, f32[192,3072]{1,0:T(8,128)}, u32[]{:S(2)}, u32[]{:S(2)}) %collective-permute-start.3) | collective-permute-done | bytes 2359328 | tf_op jit(solution)/shard_map/ppermute | solution.py:57
  74.9 3.4 collective-permute-start.1
  78.3 39.0 %collective-permute-done.9 = f32[192,3072]{1,0:T(8,128)} collective-permute-done((f32[192,3072]{1,0:T(8,128)}, f32[192,3072]{1,0:T(8,128)}, u32[]{:S(2)}, u32[]{:S(2)}) %collective-permute-start.9) | collective-permute-done | bytes 2359328 | tf_op jit(solution)/shard_map/ppermute | solution.py:57
  120.3 5.2 %fusion.46 = (f32[192,3072]{1,0:T(8,128)}, f32[192,3072]{1,0:T(8,128)}) fusion(f32[192,3072]{1,0:T(8,128)} %collective-permute-done.9, f32[192,1536]{1,0:T(8,128)S(1)} %get-tuple-element.30, f32[192,1536]{1,0:T(8,128)S(1)} %pad.15, pred[]{:T(512)S(6)} %eq.38, f32[192,3072]{1,0:T(8,128)} %collective-permute-done.6, pred[]{:T(512)S(6)} %eq.40), kind=kLoop, calls=%fused_computation.64 | loop fusion | flops 1769472 | bytes 11796482 | tf_op jit(solution)/shard_map/jit(_where)/select_n | solution.py:83
  127.4 3.8 collective-permute-start.7
  131.3 5.5 %fusion.8 = f32[192,504]{1,0:T(8,128)} fusion(f32[504,9192]{1,0:T(8,128)S(1)} %bitcast.41, f32[192,3072]{1,0:T(8,128)} %collective-permute-done, f32[192,3072]{1,0:T(8,128)} %collective-permute-done.3, pred[]{:T(512)S(6)} %lt.20), kind=kOutput, calls=%fused_computation.8 | convolution fusion | flops 1784217600 | bytes 11298817 | tf_op jit(solution)/shard_map/dot_general | solution.py:24
  136.8 5.5 %fusion.12 = f32[192,504]{1,0:T(8,128)} fusion(f32[504,9192]{1,0:T(8,128)S(1)} %bitcast.41, f32[192,3072]{1,0:T(8,128)} %collective-permute-done.3, f32[192,3072]{1,0:T(8,128)} %collective-permute-done, pred[]{:T(512)S(6)} %lt.20), kind=kOutput, calls=%fused_computation.12 | convolution fusion | flops 1784217600 | bytes 11298817 | tf_op jit(solution)/shard_map/dot_general | solution.py:24
  142.3 5.5 %fusion = f32[192,504]{1,0:T(8,128)} fusion(f32[504,9192]{1,0:T(8,128)S(1)} %bitcast.41, f32[192,3072]{1,0:T(8,128)} %collective-permute-done.6, f32[192,3072]{1,0:T(8,128)} %collective-permute-done.9, pred[]{:T(512)S(6)} %lt.20), kind=kOutput, calls=%fused_computation | convolution fusion | flops 1784217600 | bytes 11298817 | tf_op jit(solution)/shard_map/dot_general | solution.py:24
  147.8 5.5 %fusion.4 = f32[192,504]{1,0:T(8,128)} fusion(f32[504,9192]{1,0:T(8,128)S(1)} %bitcast.41, f32[192,3072]{1,0:T(8,128)} %collective-permute-done.9, f32[192,3072]{1,0:T(8,128)} %collective-permute-done.6, pred[]{:T(512)S(6)} %lt.20), kind=kOutput, calls=%fused_computation.4 | convolution fusion | flops 1784217600 | bytes 11298817 | tf_op jit(solution)/shard_map/dot_general | solution.py:24
  153.2 14.6 %collective-permute-done.4 = f32[192,3072]{1,0:T(8,128)S(1)} collective-permute-done((f32[192,3072]{1,0:T(8,128)S(1)}, f32[192,3072]{1,0:T(8,128)S(1)}, u32[]{:S(2)}, u32[]{:S(2)}) %collective-permute-start.4) | collective-permute-done | bytes 2359328 | tf_op jit(solution)/shard_map/ppermute | solution.py:57
  173.4 8.3 %fusion.39 = (f32[192,3072]{1,0:T(8,128)}, f32[192,3072]{1,0:T(8,128)}, f32[192,3072]{1,0:T(8,128)}) fusion(f32[192,3072]{1,0:T(8,128)} %copy-done.3, f32[192,1536]{1,0:T(8,128)} %slice.205, f32[192,1536]{1,0:T(8,128)} %slice.208, f32[192,1536]{1,0:T(8,128)} %pad_slice_fusion.4, f32[192,1536]{1,0:T(8,128)} %get-tuple-element.14, pred[]{:T(512)S(6)} %eq.42, ...), kind=kLoop, calls=%fused_computation.53 | loop fusion | flops 4718592 | bytes 17694724 | tf_op jit(solution)/shard_map/jit(_where)/select_n | solution.py:95
  183.9 3.6 collective-permute-start.2
  187.6 7.0 %fusion.10 = f32[192,504]{1,0:T(8,128)} fusion(f32[504,9192]{1,0:T(8,128)} %param.6, f32[192,3072]{1,0:T(8,128)} %copy-done.4, f32[192,3072]{1,0:T(8,128)} %copy-done.3, pred[]{:T(512)S(6)} %lt.20), kind=kOutput, calls=%fused_computation.10 | convolution fusion | flops 1784217600 | bytes 11298817 | tf_op jit(solution)/shard_map/dot_general | solution.py:24
  198.1 20.4 %collective-permute-done.10 = f32[192,3072]{1,0:T(8,128)} collective-permute-done((f32[192,3072]{1,0:T(8,128)}, f32[192,3072]{1,0:T(8,128)}, u32[]{:S(2)}, u32[]{:S(2)}) %collective-permute-start.10) | collective-permute-done | bytes 2359328 | tf_op jit(solution)/shard_map/ppermute | solution.py:57
  221.4 5.2 %fusion.2 = f32[192,504]{1,0:T(8,128)} fusion(f32[504,9192]{1,0:T(8,128)S(1)} %bitcast.43, f32[192,3072]{1,0:T(8,128)} %collective-permute-done.7, f32[192,3072]{1,0:T(8,128)} %collective-permute-done.10, pred[]{:T(512)S(6)} %lt.20), kind=kOutput, calls=%fused_computation.2 | convolution fusion | flops 1784217600 | bytes 11298817 | tf_op jit(solution)/shard_map/dot_general | solution.py:24
  231.3 8.3 %fusion.35 = (f32[192,3072]{1,0:T(8,128)}, f32[192,3072]{1,0:T(8,128)}, f32[192,3072]{1,0:T(8,128)}) fusion(f32[192,3072]{1,0:T(8,128)} %collective-permute-done.10, f32[192,1536]{1,0:T(8,128)} %copy-done.5, f32[192,1536]{1,0:T(8,128)} %slice.213, f32[192,1536]{1,0:T(8,128)} %get-tuple-element.29, f32[192,1536]{1,0:T(8,128)} %get-tuple-element.28, ...), kind=kLoop, calls=%fused_computation.49 | loop fusion | flops 4718592 | bytes 17694724 | tf_op jit(solution)/shard_map/jit(_where)/select_n | solution.py:95
  239.6 3.2 slice.225
  247.1 3.8 collective-permute-start.8
  250.9 18.1 %collective-permute-done.5 = f32[192,3072]{1,0:T(8,128)} collective-permute-done((f32[192,3072]{1,0:T(8,128)}, f32[192,3072]{1,0:T(8,128)}, u32[]{:S(2)}, u32[]{:S(2)}) %collective-permute-start.5) | collective-permute-done | bytes 2359328 | tf_op jit(solution)/shard_map/ppermute | solution.py:57
  280.9 4.0 fusion.16
  290.1 29.5 %collective-permute-done.11 = f32[192,3072]{1,0:T(8,128)} collective-permute-done((f32[192,3072]{1,0:T(8,128)}, f32[192,3072]{1,0:T(8,128)}, u32[]{:S(2)}, u32[]{:S(2)}) %collective-permute-start.11) | collective-permute-done | bytes 2359328 | tf_op jit(solution)/shard_map/ppermute | solution.py:57
  325.5 6.5 %fusion.6 = f32[192,504]{1,0:T(8,128)} fusion(f32[192,3072]{1,0:T(8,128)S(1)} %get-tuple-element.21, f32[504,9192]{1,0:T(8,128)} %param.6), kind=kOutput, calls=%fused_computation.6 | convolution fusion | flops 1783627776 | bytes 8939520 | tf_op jit(solution)/shard_map/dot_general | solution.py:24
  335.2 4.0 fusion.20
  348.4 46.4 %reduce-scatter.2.cloned.1.call-done = f32[1,2,2,48,504]{4,3,2,1,0:T(8,128)} async-done(((f32[8,2,2,48,504]{4,3,2,1,0:T(8,128)}), f32[1,2,2,48,504]{4,3,2,1,0:T(8,128)}) %reduce-scatter.2.cloned.1.call-update) | async-done | bytes 387088 | tf_op jit(solution)/shard_map/reduce_scatter | solution.py:134
  401.5 9.5 %collective-permute-done.13 = f32[2,48,504]{2,1,0:T(8,128)S(1)} collective-permute-done((f32[2,48,504]{2,1,0:T(8,128)S(1)}, f32[2,48,504]{2,1,0:T(8,128)S(1)}, u32[]{:S(2)}, u32[]{:S(2)}) %collective-permute-start.13) | collective-permute-done | bytes 193568 | tf_op jit(solution)/shard_map/ppermute | solution.py:146
  411.0 8.0 %collective-permute-done.12 = f32[2,48,504]{2,1,0:T(8,128)S(1)} collective-permute-done((f32[2,48,504]{2,1,0:T(8,128)S(1)}, f32[2,48,504]{2,1,0:T(8,128)S(1)}, u32[]{:S(2)}, u32[]{:S(2)}) %collective-permute-start.12) | collective-permute-done | bytes 193568 | tf_op jit(solution)/shard_map/ppermute | solution.py:147
  (163 shorter events, 92.7 us)
Async XLA Ops:
  7.2 387.6 %reduce-scatter.2.cloned.1.call-start = ((), (), s32[]{:S(2)}) async-start(), calls=%async_computation.1 | async-start | bytes 3538944 | tf_op jit(solution)/shard_map/reduce_scatter | solution.py:134
  12.4 54.3 %collective-permute-start.3 = (f32[192,3072]{1,0:T(8,128)}, f32[192,3072]{1,0:T(8,128)}, u32[]{:S(2)}, u32[]{:S(2)}) collective-permute-start(f32[192,3072]{1,0:T(8,128)} %get-tuple-element.16), channel_id=1, source_target_pairs={{0,8},{8,16},{16,24},{1,9},{9,17},{17,25},{2,10},{10,18},{18,26},{... | collective-permute-start | bytes 7077896 | tf_op jit(solution)/shard_map/ppermute | solution.py:57
  15.6 54.1 %collective-permute-start = (f32[192,3072]{1,0:T(8,128)}, f32[192,3072]{1,0:T(8,128)}, u32[]{:S(2)}, u32[]{:S(2)}) collective-permute-start(f32[192,3072]{1,0:T(8,128)} %get-tuple-element.16), channel_id=1, source_target_pairs={{24,16},{16,8},{8,0},{25,17},{17,9},{9,1},{26,18},{18,10},{10,2},{... | collective-permute-start | bytes 7077896 | tf_op jit(solution)/shard_map/ppermute | solution.py:58
  17.7 99.6 %collective-permute-start.9 = (f32[192,3072]{1,0:T(8,128)}, f32[192,3072]{1,0:T(8,128)}, u32[]{:S(2)}, u32[]{:S(2)}) collective-permute-start(f32[192,3072]{1,0:T(8,128)} %get-tuple-element.17), channel_id=1, source_target_pairs={{0,8},{8,16},{16,24},{1,9},{9,17},{17,25},{2,10},{10,18},{18,26},{... | collective-permute-start | bytes 7077896 | tf_op jit(solution)/shard_map/ppermute | solution.py:57
  22.3 98.0 %collective-permute-start.6 = (f32[192,3072]{1,0:T(8,128)}, f32[192,3072]{1,0:T(8,128)}, u32[]{:S(2)}, u32[]{:S(2)}) collective-permute-start(f32[192,3072]{1,0:T(8,128)} %get-tuple-element.17), channel_id=1, source_target_pairs={{24,16},{16,8},{8,0},{25,17},{17,9},{9,1},{26,18},{18,10},{10,2},{... | collective-permute-start | bytes 7077896 | tf_op jit(solution)/shard_map/ppermute | solution.py:58
  47.8 72.4 %copy-start.5 = (f32[192,1536]{1,0:T(8,128)}, f32[192,1536]{1,0:T(8,128)S(1)}, u32[]{:S(2)}) copy-start(f32[192,1536]{1,0:T(8,128)S(1)} %pad.15) | copy-start | bytes 3538948
  47.8 83.4 %slice-start = ((s8[18579456]{0:T(1024)(128)(4,1)}), s8[4194304]{0:T(1024)(128)(4,1)S(1)}, s32[]{:S(2)}) async-start(s8[18579456]{0:T(1024)(128)(4,1)} %bitcast.40), calls=%async_computation.2 | async-start | bytes 8388608
  49.0 82.3 %slice-start.1 = ((s8[18579456]{0:T(1024)(128)(4,1)}), s8[4194304]{0:T(1024)(128)(4,1)S(1)}, s32[]{:S(2)}) async-start(s8[18579456]{0:T(1024)(128)(4,1)} %bitcast.40), calls=%async_computation.3 | async-start | bytes 8388608
  50.7 19.0 %copy-start.7 = (f32[192,1536]{1,0:T(8,128)S(1)}, f32[192,1536]{1,0:T(8,128)}, u32[]{:S(2)}) copy-start(f32[192,1536]{1,0:T(8,128)} %slice.205) | copy-start | bytes 3538948
  69.7 61.6 %slice-start.2 = ((s8[18579456]{0:T(1024)(128)(4,1)}), s8[4194304]{0:T(1024)(128)(4,1)S(1)}, s32[]{:S(2)}) async-start(s8[18579456]{0:T(1024)(128)(4,1)} %bitcast.40), calls=%async_computation.4 | async-start | bytes 8388608
  69.7 61.6 %slice-start.3 = ((s8[18579456]{0:T(1024)(128)(4,1)}), s8[4194304]{0:T(1024)(128)(4,1)S(1)}, s32[]{:S(2)}) async-start(s8[18579456]{0:T(1024)(128)(4,1)} %bitcast.40), calls=%async_computation.5 | async-start | bytes 8388608
  72.9 94.9 %collective-permute-start.4 = (f32[192,3072]{1,0:T(8,128)S(1)}, f32[192,3072]{1,0:T(8,128)S(1)}, u32[]{:S(2)}, u32[]{:S(2)}) collective-permute-start(f32[192,3072]{1,0:T(8,128)S(1)} %get-tuple-element.40), channel_id=1, source_target_pairs={{0,8},{8,16},{16,24},{1,9},{9,17},{17,25},{2,10},{10,18},{18,26},{... | collective-permute-start | bytes 7077896 | tf_op jit(solution)/shard_map/ppermute | solution.py:57
  74.9 95.9 %collective-permute-start.1 = (f32[192,3072]{1,0:T(8,128)S(1)}, f32[192,3072]{1,0:T(8,128)S(1)}, u32[]{:S(2)}, u32[]{:S(2)}) collective-permute-start(f32[192,3072]{1,0:T(8,128)S(1)} %get-tuple-element.41), channel_id=1, source_target_pairs={{24,16},{16,8},{8,0},{25,17},{17,9},{9,1},{26,18},{18,10},{10,2},{... | collective-permute-start | bytes 7077896 | tf_op jit(solution)/shard_map/ppermute | solution.py:58
  125.5 92.9 %collective-permute-start.10 = (f32[192,3072]{1,0:T(8,128)}, f32[192,3072]{1,0:T(8,128)}, u32[]{:S(2)}, u32[]{:S(2)}) collective-permute-start(f32[192,3072]{1,0:T(8,128)} %get-tuple-element.44), channel_id=1, source_target_pairs={{0,8},{8,16},{16,24},{1,9},{9,17},{17,25},{2,10},{10,18},{18,26},{... | collective-permute-start | bytes 7077896 | tf_op jit(solution)/shard_map/ppermute | solution.py:57
  127.4 94.0 %collective-permute-start.7 = (f32[192,3072]{1,0:T(8,128)}, f32[192,3072]{1,0:T(8,128)}, u32[]{:S(2)}, u32[]{:S(2)}) collective-permute-start(f32[192,3072]{1,0:T(8,128)} %get-tuple-element.45), channel_id=1, source_target_pairs={{24,16},{16,8},{8,0},{25,17},{17,9},{9,1},{26,18},{18,10},{10,2},{... | collective-permute-start | bytes 7077896 | tf_op jit(solution)/shard_map/ppermute | solution.py:58
  167.8 27.9 %slice-start.5 = ((s8[18579456]{0:T(1024)(128)(4,1)}), s8[1802240]{0:T(1024)(128)(4,1)S(1)}, s32[]{:S(2)}) async-start(s8[18579456]{0:T(1024)(128)(4,1)} %bitcast.42), calls=%async_computation.7 | async-start | bytes 3604480
  173.4 22.3 %slice-start.6 = ((s8[18579456]{0:T(1024)(128)(4,1)}), s8[4194304]{0:T(1024)(128)(4,1)S(1)}, s32[]{:S(2)}) async-start(s8[18579456]{0:T(1024)(128)(4,1)} %bitcast.42), calls=%async_computation.8 | async-start | bytes 8388608
  173.4 22.3 %slice-start.7 = ((s8[18579456]{0:T(1024)(128)(4,1)}), s8[4194304]{0:T(1024)(128)(4,1)S(1)}, s32[]{:S(2)}) async-start(s8[18579456]{0:T(1024)(128)(4,1)} %bitcast.42), calls=%async_computation.9 | async-start | bytes 8388608
  173.4 22.3 %slice-start.8 = ((s8[18579456]{0:T(1024)(128)(4,1)}), s8[4194304]{0:T(1024)(128)(4,1)S(1)}, s32[]{:S(2)}) async-start(s8[18579456]{0:T(1024)(128)(4,1)} %bitcast.42), calls=%async_computation.10 | async-start | bytes 8388608
  181.7 87.3 %collective-permute-start.5 = (f32[192,3072]{1,0:T(8,128)}, f32[192,3072]{1,0:T(8,128)}, u32[]{:S(2)}, u32[]{:S(2)}) collective-permute-start(f32[192,3072]{1,0:T(8,128)} %get-tuple-element.22), channel_id=1, source_target_pairs={{0,8},{8,16},{16,24},{1,9},{9,17},{17,25},{2,10},{10,18},{18,26},{... | collective-permute-start | bytes 7077896 | tf_op jit(solution)/shard_map/ppermute | solution.py:57
  183.9 88.0 %collective-permute-start.2 = (f32[192,3072]{1,0:T(8,128)}, f32[192,3072]{1,0:T(8,128)}, u32[]{:S(2)}, u32[]{:S(2)}) collective-permute-start(f32[192,3072]{1,0:T(8,128)} %get-tuple-element.23), channel_id=1, source_target_pairs={{24,16},{16,8},{8,0},{25,17},{17,9},{9,1},{26,18},{18,10},{10,2},{... | collective-permute-start | bytes 7077896 | tf_op jit(solution)/shard_map/ppermute | solution.py:58
  231.3 43.6 %slice-start.10 = ((s8[18579456]{0:T(1024)(128)(4,1)}), s8[1802240]{0:T(1024)(128)(4,1)S(1)}, s32[]{:S(2)}) async-start(s8[18579456]{0:T(1024)(128)(4,1)} %bitcast.44), calls=%async_computation.12 | async-start | bytes 3604480
  231.3 43.6 %slice-start.11 = ((s8[18579456]{0:T(1024)(128)(4,1)}), s8[4194304]{0:T(1024)(128)(4,1)S(1)}, s32[]{:S(2)}) async-start(s8[18579456]{0:T(1024)(128)(4,1)} %bitcast.44), calls=%async_computation.13 | async-start | bytes 8388608
  231.3 43.6 %slice-start.12 = ((s8[18579456]{0:T(1024)(128)(4,1)}), s8[4194304]{0:T(1024)(128)(4,1)S(1)}, s32[]{:S(2)}) async-start(s8[18579456]{0:T(1024)(128)(4,1)} %bitcast.44), calls=%async_computation.14 | async-start | bytes 8388608
  242.8 32.2 %slice-start.13 = ((s8[18579456]{0:T(1024)(128)(4,1)}), s8[4194304]{0:T(1024)(128)(4,1)S(1)}, s32[]{:S(2)}) async-start(s8[18579456]{0:T(1024)(128)(4,1)} %bitcast.44), calls=%async_computation.15 | async-start | bytes 8388608
  245.1 74.4 %collective-permute-start.11 = (f32[192,3072]{1,0:T(8,128)}, f32[192,3072]{1,0:T(8,128)}, u32[]{:S(2)}, u32[]{:S(2)}) collective-permute-start(f32[192,3072]{1,0:T(8,128)} %get-tuple-element.25), channel_id=1, source_target_pairs={{0,8},{8,16},{16,24},{1,9},{9,17},{17,25},{2,10},{10,18},{18,26},{... | collective-permute-start | bytes 7077896 | tf_op jit(solution)/shard_map/ppermute | solution.py:57
  247.0 27.9 %slice-start.14 = ((s8[18579456]{0:T(1024)(128)(4,1)}), s8[4194304]{0:T(1024)(128)(4,1)S(1)}, s32[]{:S(2)}) async-start(s8[18579456]{0:T(1024)(128)(4,1)} %bitcast.44), calls=%async_computation.16 | async-start | bytes 8388608
  247.1 75.4 %collective-permute-start.8 = (f32[192,3072]{1,0:T(8,128)}, f32[192,3072]{1,0:T(8,128)}, u32[]{:S(2)}, u32[]{:S(2)}) collective-permute-start(f32[192,3072]{1,0:T(8,128)} %get-tuple-element.26), channel_id=1, source_target_pairs={{24,16},{16,8},{8,0},{25,17},{17,9},{9,1},{26,18},{18,10},{10,2},{... | collective-permute-start | bytes 7077896 | tf_op jit(solution)/shard_map/ppermute | solution.py:58
  347.5 53.6 %copy-start.29 = (f32[384]{0:T(512)S(1)}, f32[384]{0:T(512)}, u32[]{:S(2)}) copy-start(f32[384]{0:T(512)} %param.9) | copy-start | bytes 4612
  347.5 53.8 %copy-start.30 = (f32[64]{0:T(128)S(1)}, f32[64]{0:T(128)}, u32[]{:S(2)}) copy-start(f32[64]{0:T(128)} %param.8) | copy-start | bytes 772
  395.9 15.1 %collective-permute-start.13 = (f32[2,48,504]{2,1,0:T(8,128)S(1)}, f32[2,48,504]{2,1,0:T(8,128)S(1)}, u32[]{:S(2)}, u32[]{:S(2)}) collective-permute-start(f32[2,48,504]{2,1,0:T(8,128)S(1)} %get-tuple-element.58), channel_id=1, source_target_pairs={{0,0},{4,16},{8,8},{12,24},{16,4},{20,20},{24,12},{28,28},{1,1},{5... | collective-permute-start | bytes 580616 | tf_op jit(solution)/shard_map/ppermute | solution.py:146
  398.9 20.1 %collective-permute-start.12 = (f32[2,48,504]{2,1,0:T(8,128)S(1)}, f32[2,48,504]{2,1,0:T(8,128)S(1)}, u32[]{:S(2)}, u32[]{:S(2)}) collective-permute-start(f32[2,48,504]{2,1,0:T(8,128)S(1)} %get-tuple-element.59), channel_id=1, source_target_pairs={{0,8},{4,24},{8,0},{12,16},{16,12},{20,28},{24,4},{28,20},{1,9},{5... | collective-permute-start | bytes 580616 | tf_op jit(solution)/shard_map/ppermute | solution.py:147
  (30 other events, 117.8 us)
Sparse Core Ops, SparseCore 0:
  347.7 47.0 reduce-scatter.1

commit v2 on v1

--- a/solution.py
+++ b/solution.py
@@ -36,6 +36,13 @@
 
 def settled(value):
     return lax.optimization_barrier(value)
+
+
+def halves(blocks, dim, upper, axis, swap):
+    low_half = lax.index_in_dim(blocks, 0, dim, keepdims=False)
+    high_half = lax.index_in_dim(blocks, 1, dim, keepdims=False)
+    given = jnp.where(upper, low_half, high_half)
+    return jnp.where(upper, high_half, low_half) + lax.ppermute(given, axis, swap)
 
 
 def line_exchange(amplitudes, integrals):
@@ -129,9 +136,20 @@
     both = [jnp.where(low, both[at], both[3 - at]) for at in range(4)]
     layers = lax.axis_size("layer")
     slab = width // layers
-    stacked = jnp.stack(both).reshape(2, 2, 2, layers, slab, pair_rows)
-    stacked = stacked.transpose(0, 3, 1, 2, 4, 5).reshape(-1, 2, 2, slab, pair_rows)
-    mine = lax.psum_scatter(stacked, ("col", "layer"), scatter_dimension=0, tiled=True)[0]
+    stacked = jnp.stack(both).reshape(2, 2, 2, 2, 2, slab, pair_rows)
+    layer = lax.axis_index("layer")
+    upper_col = lax.axis_index("col") == 1
+    upper_pair = layer // 2 == 1
+    pair_swap = [(0, 2), (2, 0), (1, 3), (3, 1)]
+    core_swap = [(0, 1), (1, 0), (2, 3), (3, 2)]
+    col_swap = [(0, 1), (1, 0)]
+    halved = halves(stacked, 4, layer % 2 == 1, "layer", core_swap)
+    pair_first = halves(halved[:, 0], 2, upper_pair, "layer", pair_swap)
+    col_first = halves(halved[:, 1], 0, upper_col, "col", col_swap)
+    mine = (
+        halves(pair_first, 0, upper_col, "col", col_swap),
+        halves(col_first, 1, upper_pair, "layer", pair_swap),
+    )
     odd = row % 2 == 1
     same = jnp.where(odd, mine[1], mine[0])
     other = jnp.where(odd, mine[0], mine[1])
@@ -165,6 +183,7 @@
 
 def shards(amplitudes, integrals, occ_energy, vir_energy):
     in_line = lax.axis_size("row") == 4 and lax.axis_size("col") == 2
+    in_line = in_line and lax.axis_size("layer") == 4
     fits = amplitudes.shape[0] <= 3 * integrals.shape[1]
     depth = integrals.shape[0]
     if in_line and fits and depth > 5 * near_depth(depth):

time: 434 us -> 394 us (0.908)
  the two profiles are of different devices: /device:TPU:17 before, /device:TPU:4 now
where the time goes in v2:
time: 394 us; the launch traced here: 388 us
  waiting for transfers between devices  186 us (47%)
  matrix products  72.9 us (19%)
  local copies, waits for them, and re-layouts  45.2 us (11%)
  starting transfers between devices  42.9 us (11%)
  other arithmetic  39.6 us (10%)
    ppermute x6, waiting for transfers between devices, shift(): lax.ppermute(up_payload, 'row', up_pairs)  121 us
    dot_general x15, matrix products, contract(): lax.dot_general(columns, rows, (((1,), (1,)), ((), ())), precision=lax.Pr...  72.9 us
    ppermute x6, waiting for transfers between devices, shift(): lax.ppermute(down_payload, 'row', down_pairs)  33.5 us
    ppermute x6, starting transfers between devices, shift(): lax.ppermute(up_payload, 'row', up_pairs)  25.3 us
    ppermute x5, waiting for transfers between devices, halves(): lax.ppermute(given, axis, swap)  17.8 us
    select_n x2, other arithmetic, line_exchange(): jnp.where(row == 0, edge3, jnp.where(row == 1, up_mid, up2))  16.6 us
    ppermute x6, starting transfers between devices, shift(): lax.ppermute(down_payload, 'row', down_pairs)  8.9 us
    unnamed x96, local copies, waits for them, and re-layouts  8.79 us
  transfers between devices with their start and end apart: 19, of which 18 were waited for; matrix products, arithmetic and copies ran while one was open for 32% of the time, Pallas kernels for 0%

profile of v2, /device:TPU:4, one launch (start us, length us, event | category | flops | bytes accessed | tf_op | source)
XLA Modules:
  0.0 388.0 jit_solution(13634472616881530810)
XLA Ops:
  0.6 5.2 %fusion.85 = (f32[192,3072]{1,0:T(8,128)}, f32[192,3072]{1,0:T(8,128)}) fusion(f32[192,9192]{1,0:T(8,128)} %bitcast.77), kind=kLoop, calls=%fused_computation.154 | loop fusion | bytes 9437184 | tf_op jit(solution)/shard_map/slice | solution.py:58
  5.9 4.9 %collective-permute-start.3 = (f32[192,3072]{1,0:T(8,128)}, f32[192,3072]{1,0:T(8,128)}, u32[]{:S(2)}, u32[]{:S(2)}) collective-permute-start(f32[192,3072]{1,0:T(8,128)} %get-tuple-element.19), channel_id=1, source_target_pairs={{0,8},{8,16},{16,24},{1,9},{9,17},{17,25},{2,10},{10,18},{18,26},{... | collective-permute-start | bytes 7077896 | tf_op jit(solution)/shard_map/ppermute | solution.py:64
  12.1 6.0 %collective-permute-start.9 = (f32[192,3072]{1,0:T(8,128)}, f32[192,3072]{1,0:T(8,128)}, u32[]{:S(2)}, u32[]{:S(2)}) collective-permute-start(f32[192,3072]{1,0:T(8,128)} %get-tuple-element.20), channel_id=1, source_target_pairs={{0,8},{8,16},{16,24},{1,9},{9,17},{17,25},{2,10},{10,18},{18,26},{... | collective-permute-start | bytes 7077896 | tf_op jit(solution)/shard_map/ppermute | solution.py:64
  19.3 12.9 %fusion.93 = f32[192,504]{1,0:T(8,128)} fusion(f32[9192,192]{0,1:T(8,128)S(1)} %copy-done.2, f32[504,9192]{1,0:T(8,128)} %param.6), kind=kOutput, calls=%fused_computation.162 | convolution fusion | flops 5336948736 | bytes 25977600 | tf_op jit(solution)/shard_map/dot_general | solution.py:24
  49.4 11.9 %collective-permute-done.3 = f32[192,3072]{1,0:T(8,128)} collective-permute-done((f32[192,3072]{1,0:T(8,128)}, f32[192,3072]{1,0:T(8,128)}, u32[]{:S(2)}, u32[]{:S(2)}) %collective-permute-start.3) | collective-permute-done | bytes 2359328 | tf_op jit(solution)/shard_map/ppermute | solution.py:64
  61.3 5.8 %collective-permute-done = f32[192,3072]{1,0:T(8,128)} collective-permute-done((f32[192,3072]{1,0:T(8,128)}, f32[192,3072]{1,0:T(8,128)}, u32[]{:S(2)}, u32[]{:S(2)}) %collective-permute-start) | collective-permute-done | bytes 2359328 | tf_op jit(solution)/shard_map/ppermute | solution.py:65
  73.9 37.9 %collective-permute-done.9 = f32[192,3072]{1,0:T(8,128)} collective-permute-done((f32[192,3072]{1,0:T(8,128)}, f32[192,3072]{1,0:T(8,128)}, u32[]{:S(2)}, u32[]{:S(2)}) %collective-permute-start.9) | collective-permute-done | bytes 2359328 | tf_op jit(solution)/shard_map/ppermute | solution.py:64
  111.8 5.8 %collective-permute-done.6 = f32[192,3072]{1,0:T(8,128)} collective-permute-done((f32[192,3072]{1,0:T(8,128)}, f32[192,3072]{1,0:T(8,128)}, u32[]{:S(2)}, u32[]{:S(2)}) %collective-permute-start.6) | collective-permute-done | bytes 2359328 | tf_op jit(solution)/shard_map/ppermute | solution.py:65
  117.7 4.6 %fusion.46 = (f32[192,3072]{1,0:T(8,128)}, f32[192,3072]{1,0:T(8,128)}) fusion(f32[192,3072]{1,0:T(8,128)} %collective-permute-done.9, f32[192,1536]{1,0:T(8,128)S(1)} %get-tuple-element.35, f32[192,1536]{1,0:T(8,128)S(1)} %pad.15, pred[]{:T(512)S(6)} %eq.49, f32[192,3072]{1,0:T(8,128)} %collective-permute-done.6, pred[]{:T(512)S(6)} %eq.96), kind=kLoop, calls=%fused_computation.64 | loop fusion | flops 1769472 | bytes 11796482 | tf_op jit(solution)/shard_map/jit(_where)/select_n | solution.py:90
  122.2 4.2 %collective-permute-start.10 = (f32[192,3072]{1,0:T(8,128)}, f32[192,3072]{1,0:T(8,128)}, u32[]{:S(2)}, u32[]{:S(2)}) collective-permute-start(f32[192,3072]{1,0:T(8,128)} %get-tuple-element.49), channel_id=1, source_target_pairs={{0,8},{8,16},{16,24},{1,9},{9,17},{17,25},{2,10},{10,18},{18,26},{... | collective-permute-start | bytes 7077896 | tf_op jit(solution)/shard_map/ppermute | solution.py:64
  128.3 5.5 %fusion.8 = f32[192,504]{1,0:T(8,128)} fusion(f32[504,9192]{1,0:T(8,128)S(1)} %bitcast.72, f32[192,3072]{1,0:T(8,128)} %collective-permute-done, f32[192,3072]{1,0:T(8,128)} %collective-permute-done.3, pred[]{:T(512)S(6)} %lt.25), kind=kOutput, calls=%fused_computation.8 | convolution fusion | flops 1784217600 | bytes 11298817 | tf_op jit(solution)/shard_map/dot_general | solution.py:24
  133.7 5.4 %fusion.12 = f32[192,504]{1,0:T(8,128)} fusion(f32[504,9192]{1,0:T(8,128)S(1)} %bitcast.72, f32[192,3072]{1,0:T(8,128)} %collective-permute-done.3, f32[192,3072]{1,0:T(8,128)} %collective-permute-done, pred[]{:T(512)S(6)} %lt.25), kind=kOutput, calls=%fused_computation.12 | convolution fusion | flops 1784217600 | bytes 11298817 | tf_op jit(solution)/shard_map/dot_general | solution.py:24
  139.2 5.5 %fusion = f32[192,504]{1,0:T(8,128)} fusion(f32[504,9192]{1,0:T(8,128)S(1)} %bitcast.72, f32[192,3072]{1,0:T(8,128)} %collective-permute-done.6, f32[192,3072]{1,0:T(8,128)} %collective-permute-done.9, pred[]{:T(512)S(6)} %lt.25), kind=kOutput, calls=%fused_computation | convolution fusion | flops 1784217600 | bytes 11298817 | tf_op jit(solution)/shard_map/dot_general | solution.py:24
  144.7 5.5 %fusion.4 = f32[192,504]{1,0:T(8,128)} fusion(f32[504,9192]{1,0:T(8,128)S(1)} %bitcast.72, f32[192,3072]{1,0:T(8,128)} %collective-permute-done.9, f32[192,3072]{1,0:T(8,128)} %collective-permute-done.6, pred[]{:T(512)S(6)} %lt.25), kind=kOutput, calls=%fused_computation.4 | convolution fusion | flops 1784217600 | bytes 11298817 | tf_op jit(solution)/shard_map/dot_general | solution.py:24
  150.1 12.2 %collective-permute-done.4 = f32[192,3072]{1,0:T(8,128)S(1)} collective-permute-done((f32[192,3072]{1,0:T(8,128)S(1)}, f32[192,3072]{1,0:T(8,128)S(1)}, u32[]{:S(2)}, u32[]{:S(2)}) %collective-permute-start.4) | collective-permute-done | bytes 2359328 | tf_op jit(solution)/shard_map/ppermute | solution.py:64
  163.4 4.7 %collective-permute-done.1 = f32[192,3072]{1,0:T(8,128)S(1)} collective-permute-done((f32[192,3072]{1,0:T(8,128)S(1)}, f32[192,3072]{1,0:T(8,128)S(1)}, u32[]{:S(2)}, u32[]{:S(2)}) %collective-permute-start.1) | collective-permute-done | bytes 2359328 | tf_op jit(solution)/shard_map/ppermute | solution.py:65
  170.7 8.3 %fusion.39 = (f32[192,3072]{1,0:T(8,128)}, f32[192,3072]{1,0:T(8,128)}, f32[192,3072]{1,0:T(8,128)}) fusion(f32[192,3072]{1,0:T(8,128)} %copy-done.3, f32[192,1536]{1,0:T(8,128)} %slice.242, f32[192,1536]{1,0:T(8,128)} %slice.245, f32[192,1536]{1,0:T(8,128)} %pad_slice_fusion.4, f32[192,1536]{1,0:T(8,128)} %get-tuple-element.17, pred[]{:T(512)S(6)} %eq.98, ...), kind=kLoop, calls=%fused_computation.53 | loop fusion | flops 4718592 | bytes 17694724 | tf_op jit(solution)/shard_map/jit(_where)/select_n | solution.py:102
  184.3 7.4 %fusion.10 = f32[192,504]{1,0:T(8,128)} fusion(f32[504,9192]{1,0:T(8,128)} %param.6, f32[192,3072]{1,0:T(8,128)} %copy-done.4, f32[192,3072]{1,0:T(8,128)} %copy-done.3, pred[]{:T(512)S(6)} %lt.25), kind=kOutput, calls=%fused_computation.10 | convolution fusion | flops 1784217600 | bytes 11298817 | tf_op jit(solution)/shard_map/dot_general | solution.py:24
  195.2 17.8 %collective-permute-done.10 = f32[192,3072]{1,0:T(8,128)} collective-permute-done((f32[192,3072]{1,0:T(8,128)}, f32[192,3072]{1,0:T(8,128)}, u32[]{:S(2)}, u32[]{:S(2)}) %collective-permute-start.10) | collective-permute-done | bytes 2359328 | tf_op jit(solution)/shard_map/ppermute | solution.py:64
  213.0 5.8 %collective-permute-done.7 = f32[192,3072]{1,0:T(8,128)} collective-permute-done((f32[192,3072]{1,0:T(8,128)}, f32[192,3072]{1,0:T(8,128)}, u32[]{:S(2)}, u32[]{:S(2)}) %collective-permute-start.7) | collective-permute-done | bytes 2359328 | tf_op jit(solution)/shard_map/ppermute | solution.py:65
  218.8 5.2 %fusion.2 = f32[192,504]{1,0:T(8,128)} fusion(f32[504,9192]{1,0:T(8,128)S(1)} %bitcast.74, f32[192,3072]{1,0:T(8,128)} %collective-permute-done.7, f32[192,3072]{1,0:T(8,128)} %collective-permute-done.10, pred[]{:T(512)S(6)} %lt.25), kind=kOutput, calls=%fused_computation.2 | convolution fusion | flops 1784217600 | bytes 11298817 | tf_op jit(solution)/shard_map/dot_general | solution.py:24
  228.8 8.3 %fusion.35 = (f32[192,3072]{1,0:T(8,128)}, f32[192,3072]{1,0:T(8,128)}, f32[192,3072]{1,0:T(8,128)}) fusion(f32[192,3072]{1,0:T(8,128)} %collective-permute-done.10, f32[192,1536]{1,0:T(8,128)} %copy-done.5, f32[192,1536]{1,0:T(8,128)} %slice.250, f32[192,1536]{1,0:T(8,128)} %get-tuple-element.34, f32[192,1536]{1,0:T(8,128)} %get-tuple-element.33, ...), kind=kLoop, calls=%fused_computation.49 | loop fusion | flops 4718592 | bytes 17694724 | tf_op jit(solution)/shard_map/jit(_where)/select_n | solution.py:102
  247.8 15.7 %collective-permute-done.5 = f32[192,3072]{1,0:T(8,128)} collective-permute-done((f32[192,3072]{1,0:T(8,128)}, f32[192,3072]{1,0:T(8,128)}, u32[]{:S(2)}, u32[]{:S(2)}) %collective-permute-start.5) | collective-permute-done | bytes 2359328 | tf_op jit(solution)/shard_map/ppermute | solution.py:64
  263.5 5.8 %collective-permute-done.2 = f32[192,3072]{1,0:T(8,128)} collective-permute-done((f32[192,3072]{1,0:T(8,128)}, f32[192,3072]{1,0:T(8,128)}, u32[]{:S(2)}, u32[]{:S(2)}) %collective-permute-start.2) | collective-permute-done | bytes 2359328 | tf_op jit(solution)/shard_map/ppermute | solution.py:65
  278.3 4.0 %fusion.16 = f32[576,504]{1,0:T(8,128)} fusion(f32[384,1536]{1,0:T(8,128)S(1)} %maximum_select_fusion, f32[192,1536]{1,0:T(8,128)S(1)} %copy-done.8, f32[192,1536]{1,0:T(8,128)S(1)} %get-tuple-element.40, f32[192,1536]{1,0:T(8,128)S(1)} %get-tuple-element.39, f32[192,1536]{1,0:T(8,128)S(1)} %copy-done.26, pred[]{:T(512)S(6)} %or.3), kind=kOutput, calls=%fused_computation.20 | convolution fusion | flops 2678648832 | bytes 8239105 | tf_op jit(solution)/shard_map/dot_general | solution.py:24
  287.5 25.4 %collective-permute-done.11 = f32[192,3072]{1,0:T(8,128)} collective-permute-done((f32[192,3072]{1,0:T(8,128)}, f32[192,3072]{1,0:T(8,128)}, u32[]{:S(2)}, u32[]{:S(2)}) %collective-permute-start.11) | collective-permute-done | bytes 2359328 | tf_op jit(solution)/shard_map/ppermute | solution.py:64
  312.9 5.5 %collective-permute-done.8 = f32[192,3072]{1,0:T(8,128)} collective-permute-done((f32[192,3072]{1,0:T(8,128)}, f32[192,3072]{1,0:T(8,128)}, u32[]{:S(2)}, u32[]{:S(2)}) %collective-permute-start.8) | collective-permute-done | bytes 2359328 | tf_op jit(solution)/shard_map/ppermute | solution.py:65
  321.5 6.5 %fusion.6 = f32[192,504]{1,0:T(8,128)} fusion(f32[192,3072]{1,0:T(8,128)S(1)} %get-tuple-element.24, f32[504,9192]{1,0:T(8,128)} %param.6), kind=kOutput, calls=%fused_computation.6 | convolution fusion | flops 1783627776 | bytes 8939520 | tf_op jit(solution)/shard_map/dot_general | solution.py:24
  351.5 8.9 %collective-permute-done.15 = f32[2,2,48,504]{3,2,0,1:T(8,128)S(1)} collective-permute-done((f32[2,2,48,504]{3,2,0,1:T(8,128)S(1)}, f32[2,2,48,504]{3,2,0,1:T(8,128)S(1)}, u32[]{:S(2)}, u32[]{:S(2)}) %collective-permute-start.15) | collective-permute-done | bytes 387104 | tf_op jit(solution)/shard_map/ppermute | solution.py:45
  368.5 4.3 %collective-permute-start.18 = (f32[2,48,504]{2,1,0:T(8,128)S(1)}, f32[2,48,504]{2,1,0:T(8,128)S(1)}, u32[]{:S(2)}, u32[]{:S(2)}) collective-permute-start(f32[2,48,504]{2,1,0:T(8,128)S(1)} %get-tuple-element.8), channel_id=1, source_target_pairs={{0,0},{4,16},{8,8},{12,24},{16,4},{20,20},{24,12},{28,28},{1,1},{5... | collective-permute-start | bytes 580616 | tf_op jit(solution)/shard_map/ppermute | solution.py:164
  373.2 5.0 %collective-permute-done.17 = f32[2,48,504]{2,1,0:T(8,128)S(1)} collective-permute-done((f32[2,48,504]{2,1,0:T(8,128)S(1)}, f32[2,48,504]{2,1,0:T(8,128)S(1)}, u32[]{:S(2)}, u32[]{:S(2)}) %collective-permute-start.17) | collective-permute-done | bytes 193568 | tf_op jit(solution)/shard_map/ppermute | solution.py:165
  378.3 8.3 %collective-permute-done.18 = f32[2,48,504]{2,1,0:T(8,128)S(1)} collective-permute-done((f32[2,48,504]{2,1,0:T(8,128)S(1)}, f32[2,48,504]{2,1,0:T(8,128)S(1)}, u32[]{:S(2)}, u32[]{:S(2)}) %collective-permute-start.18) | collective-permute-done | bytes 193568 | tf_op jit(solution)/shard_map/ppermute | solution.py:164
  (180 shorter events, 105.8 us)
Async XLA Ops:
  5.9 55.4 %collective-permute-start.3 = (f32[192,3072]{1,0:T(8,128)}, f32[192,3072]{1,0:T(8,128)}, u32[]{:S(2)}, u32[]{:S(2)}) collective-permute-start(f32[192,3072]{1,0:T(8,128)} %get-tuple-element.19), channel_id=1, source_target_pairs={{0,8},{8,16},{16,24},{1,9},{9,17},{17,25},{2,10},{10,18},{18,26},{... | collective-permute-start | bytes 7077896 | tf_op jit(solution)/shard_map/ppermute | solution.py:64
  10.8 56.3 %collective-permute-start = (f32[192,3072]{1,0:T(8,128)}, f32[192,3072]{1,0:T(8,128)}, u32[]{:S(2)}, u32[]{:S(2)}) collective-permute-start(f32[192,3072]{1,0:T(8,128)} %get-tuple-element.19), channel_id=1, source_target_pairs={{24,16},{16,8},{8,0},{25,17},{17,9},{9,1},{26,18},{18,10},{10,2},{... | collective-permute-start | bytes 7077896 | tf_op jit(solution)/shard_map/ppermute | solution.py:65
  12.1 99.8 %collective-permute-start.9 = (f32[192,3072]{1,0:T(8,128)}, f32[192,3072]{1,0:T(8,128)}, u32[]{:S(2)}, u32[]{:S(2)}) collective-permute-start(f32[192,3072]{1,0:T(8,128)} %get-tuple-element.20), channel_id=1, source_target_pairs={{0,8},{8,16},{16,24},{1,9},{9,17},{17,25},{2,10},{10,18},{18,26},{... | collective-permute-start | bytes 7077896 | tf_op jit(solution)/shard_map/ppermute | solution.py:64
  18.0 99.6 %collective-permute-start.6 = (f32[192,3072]{1,0:T(8,128)}, f32[192,3072]{1,0:T(8,128)}, u32[]{:S(2)}, u32[]{:S(2)}) collective-permute-start(f32[192,3072]{1,0:T(8,128)} %get-tuple-element.20), channel_id=1, source_target_pairs={{24,16},{16,8},{8,0},{25,17},{17,9},{9,1},{26,18},{18,10},{10,2},{... | collective-permute-start | bytes 7077896 | tf_op jit(solution)/shard_map/ppermute | solution.py:65
  42.9 74.7 %copy-start.5 = (f32[192,1536]{1,0:T(8,128)}, f32[192,1536]{1,0:T(8,128)S(1)}, u32[]{:S(2)}) copy-start(f32[192,1536]{1,0:T(8,128)S(1)} %pad.15) | copy-start | bytes 3538948
  42.9 85.3 %slice-start = ((s8[18579456]{0:T(1024)(128)(4,1)}), s8[4194304]{0:T(1024)(128)(4,1)S(1)}, s32[]{:S(2)}) async-start(s8[18579456]{0:T(1024)(128)(4,1)} %bitcast.71), calls=%async_computation | async-start | bytes 8388608
  44.1 84.2 %slice-start.1 = ((s8[18579456]{0:T(1024)(128)(4,1)}), s8[4194304]{0:T(1024)(128)(4,1)S(1)}, s32[]{:S(2)}) async-start(s8[18579456]{0:T(1024)(128)(4,1)} %bitcast.71), calls=%async_computation.1 | async-start | bytes 8388608
  67.1 61.1 %slice-start.2 = ((s8[18579456]{0:T(1024)(128)(4,1)}), s8[4194304]{0:T(1024)(128)(4,1)S(1)}, s32[]{:S(2)}) async-start(s8[18579456]{0:T(1024)(128)(4,1)} %bitcast.71), calls=%async_computation.2 | async-start | bytes 8388608
  67.1 61.1 %slice-start.3 = ((s8[18579456]{0:T(1024)(128)(4,1)}), s8[4194304]{0:T(1024)(128)(4,1)S(1)}, s32[]{:S(2)}) async-start(s8[18579456]{0:T(1024)(128)(4,1)} %bitcast.71), calls=%async_computation.3 | async-start | bytes 8388608
  69.6 92.7 %collective-permute-start.4 = (f32[192,3072]{1,0:T(8,128)S(1)}, f32[192,3072]{1,0:T(8,128)S(1)}, u32[]{:S(2)}, u32[]{:S(2)}) collective-permute-start(f32[192,3072]{1,0:T(8,128)S(1)} %get-tuple-element.45), channel_id=1, source_target_pairs={{0,8},{8,16},{16,24},{1,9},{9,17},{17,25},{2,10},{10,18},{18,26},{... | collective-permute-start | bytes 7077896 | tf_op jit(solution)/shard_map/ppermute | solution.py:64
  72.6 95.5 %collective-permute-start.1 = (f32[192,3072]{1,0:T(8,128)S(1)}, f32[192,3072]{1,0:T(8,128)S(1)}, u32[]{:S(2)}, u32[]{:S(2)}) collective-permute-start(f32[192,3072]{1,0:T(8,128)S(1)} %get-tuple-element.46), channel_id=1, source_target_pairs={{24,16},{16,8},{8,0},{25,17},{17,9},{9,1},{26,18},{18,10},{10,2},{... | collective-permute-start | bytes 7077896 | tf_op jit(solution)/shard_map/ppermute | solution.py:65
  122.2 90.7 %collective-permute-start.10 = (f32[192,3072]{1,0:T(8,128)}, f32[192,3072]{1,0:T(8,128)}, u32[]{:S(2)}, u32[]{:S(2)}) collective-permute-start(f32[192,3072]{1,0:T(8,128)} %get-tuple-element.49), channel_id=1, source_target_pairs={{0,8},{8,16},{16,24},{1,9},{9,17},{17,25},{2,10},{10,18},{18,26},{... | collective-permute-start | bytes 7077896 | tf_op jit(solution)/shard_map/ppermute | solution.py:64
  126.5 92.3 %collective-permute-start.7 = (f32[192,3072]{1,0:T(8,128)}, f32[192,3072]{1,0:T(8,128)}, u32[]{:S(2)}, u32[]{:S(2)}) collective-permute-start(f32[192,3072]{1,0:T(8,128)} %get-tuple-element.50), channel_id=1, source_target_pairs={{24,16},{16,8},{8,0},{25,17},{17,9},{9,1},{26,18},{18,10},{10,2},{... | collective-permute-start | bytes 7077896 | tf_op jit(solution)/shard_map/ppermute | solution.py:65
  162.3 30.5 %slice-start.5 = ((s8[18579456]{0:T(1024)(128)(4,1)}), s8[1802240]{0:T(1024)(128)(4,1)S(1)}, s32[]{:S(2)}) async-start(s8[18579456]{0:T(1024)(128)(4,1)} %bitcast.73), calls=%async_computation.5 | async-start | bytes 3604480
  170.7 22.1 %slice-start.7 = ((s8[18579456]{0:T(1024)(128)(4,1)}), s8[4194304]{0:T(1024)(128)(4,1)S(1)}, s32[]{:S(2)}) async-start(s8[18579456]{0:T(1024)(128)(4,1)} %bitcast.73), calls=%async_computation.7 | async-start | bytes 8388608
  170.7 22.1 %slice-start.8 = ((s8[18579456]{0:T(1024)(128)(4,1)}), s8[4194304]{0:T(1024)(128)(4,1)S(1)}, s32[]{:S(2)}) async-start(s8[18579456]{0:T(1024)(128)(4,1)} %bitcast.73), calls=%async_computation.8 | async-start | bytes 8388608
  179.0 84.5 %collective-permute-start.5 = (f32[192,3072]{1,0:T(8,128)}, f32[192,3072]{1,0:T(8,128)}, u32[]{:S(2)}, u32[]{:S(2)}) collective-permute-start(f32[192,3072]{1,0:T(8,128)} %get-tuple-element.25), channel_id=1, source_target_pairs={{0,8},{8,16},{16,24},{1,9},{9,17},{17,25},{2,10},{10,18},{18,26},{... | collective-permute-start | bytes 7077896 | tf_op jit(solution)/shard_map/ppermute | solution.py:64
  182.7 86.6 %collective-permute-start.2 = (f32[192,3072]{1,0:T(8,128)}, f32[192,3072]{1,0:T(8,128)}, u32[]{:S(2)}, u32[]{:S(2)}) collective-permute-start(f32[192,3072]{1,0:T(8,128)} %get-tuple-element.26), channel_id=1, source_target_pairs={{24,16},{16,8},{8,0},{25,17},{17,9},{9,1},{26,18},{18,10},{10,2},{... | collective-permute-start | bytes 7077896 | tf_op jit(solution)/shard_map/ppermute | solution.py:65
  228.8 43.5 %slice-start.10 = ((s8[18579456]{0:T(1024)(128)(4,1)}), s8[1802240]{0:T(1024)(128)(4,1)S(1)}, s32[]{:S(2)}) async-start(s8[18579456]{0:T(1024)(128)(4,1)} %bitcast.75), calls=%async_computation.10 | async-start | bytes 3604480
  228.8 43.5 %slice-start.11 = ((s8[18579456]{0:T(1024)(128)(4,1)}), s8[4194304]{0:T(1024)(128)(4,1)S(1)}, s32[]{:S(2)}) async-start(s8[18579456]{0:T(1024)(128)(4,1)} %bitcast.75), calls=%async_computation.11 | async-start | bytes 8388608
  228.8 43.5 %slice-start.12 = ((s8[18579456]{0:T(1024)(128)(4,1)}), s8[4194304]{0:T(1024)(128)(4,1)S(1)}, s32[]{:S(2)}) async-start(s8[18579456]{0:T(1024)(128)(4,1)} %bitcast.75), calls=%async_computation.12 | async-start | bytes 8388608
  240.3 32.1 %slice-start.13 = ((s8[18579456]{0:T(1024)(128)(4,1)}), s8[4194304]{0:T(1024)(128)(4,1)S(1)}, s32[]{:S(2)}) async-start(s8[18579456]{0:T(1024)(128)(4,1)} %bitcast.75), calls=%async_computation.13 | async-start | bytes 8388608
  242.6 70.3 %collective-permute-start.11 = (f32[192,3072]{1,0:T(8,128)}, f32[192,3072]{1,0:T(8,128)}, u32[]{:S(2)}, u32[]{:S(2)}) collective-permute-start(f32[192,3072]{1,0:T(8,128)} %get-tuple-element.28), channel_id=1, source_target_pairs={{0,8},{8,16},{16,24},{1,9},{9,17},{17,25},{2,10},{10,18},{18,26},{... | collective-permute-start | bytes 7077896 | tf_op jit(solution)/shard_map/ppermute | solution.py:64
  246.1 26.3 %slice-start.14 = ((s8[18579456]{0:T(1024)(128)(4,1)}), s8[4194304]{0:T(1024)(128)(4,1)S(1)}, s32[]{:S(2)}) async-start(s8[18579456]{0:T(1024)(128)(4,1)} %bitcast.75), calls=%async_computation.14 | async-start | bytes 8388608
  246.1 72.4 %collective-permute-start.8 = (f32[192,3072]{1,0:T(8,128)}, f32[192,3072]{1,0:T(8,128)}, u32[]{:S(2)}, u32[]{:S(2)}) collective-permute-start(f32[192,3072]{1,0:T(8,128)} %get-tuple-element.29), channel_id=1, source_target_pairs={{24,16},{16,8},{8,0},{25,17},{17,9},{9,1},{26,18},{18,10},{10,2},{... | collective-permute-start | bytes 7077896 | tf_op jit(solution)/shard_map/ppermute | solution.py:65
  343.5 3.8 collective-permute-start.12
  349.2 11.2 %collective-permute-start.15 = (f32[2,2,48,504]{3,2,0,1:T(8,128)S(1)}, f32[2,2,48,504]{3,2,0,1:T(8,128)S(1)}, u32[]{:S(2)}, u32[]{:S(2)}) collective-permute-start(f32[2,2,48,504]{3,2,0,1:T(8,128)S(1)} %select_bitcast_fusion.1), channel_id=1, source_target_pairs={{0,4},{4,0},{1,5},{5,1},{2,6},{6,2},{3,7},{7,3},{8,12},{12,8},{9,1... | collective-permute-start | bytes 1161224 | tf_op jit(solution)/shard_map/ppermute | solution.py:45
  350.0 12.2 %collective-permute-start.13 = (f32[2,2,48,504]{3,2,1,0:T(8,128)S(1)}, f32[2,2,48,504]{3,2,1,0:T(8,128)S(1)}, u32[]{:S(2)}, u32[]{:S(2)}) collective-permute-start(f32[2,2,48,504]{3,2,1,0:T(8,128)S(1)} %select_bitcast_fusion.2), channel_id=1, source_target_pairs={{0,2},{2,0},{1,3},{3,1},{4,6},{6,4},{5,7},{7,5},{8,10},{10,8},{9,1... | collective-permute-start | bytes 1161224 | tf_op jit(solution)/shard_map/ppermute | solution.py:45
  360.6 6.2 %collective-permute-start.16 = (f32[2,48,504]{2,1,0:T(8,128)S(1)}, f32[2,48,504]{2,1,0:T(8,128)S(1)}, u32[]{:S(2)}, u32[]{:S(2)}) collective-permute-start(f32[2,48,504]{2,1,0:T(8,128)S(1)} %select_bitcast_fusion.7), channel_id=1, source_target_pairs={{0,2},{2,0},{1,3},{3,1},{4,6},{6,4},{5,7},{7,5},{8,10},{10,8},{9,1... | collective-permute-start | bytes 580616 | tf_op jit(solution)/shard_map/ppermute | solution.py:45
  362.3 5.9 %collective-permute-start.14 = (f32[2,48,504]{2,1,0:T(8,128)S(1)}, f32[2,48,504]{2,1,0:T(8,128)S(1)}, u32[]{:S(2)}, u32[]{:S(2)}) collective-permute-start(f32[2,48,504]{2,1,0:T(8,128)S(1)} %select_bitcast_fusion.8), channel_id=1, source_target_pairs={{0,4},{4,0},{1,5},{5,1},{2,6},{6,2},{3,7},{7,3},{8,12},{12,8},{9,1... | collective-permute-start | bytes 580616 | tf_op jit(solution)/shard_map/ppermute | solution.py:45
  368.3 9.9 %collective-permute-start.17 = (f32[2,48,504]{2,1,0:T(8,128)S(1)}, f32[2,48,504]{2,1,0:T(8,128)S(1)}, u32[]{:S(2)}, u32[]{:S(2)}) collective-permute-start(f32[2,48,504]{2,1,0:T(8,128)S(1)} %broadcast_select_fusion.9), channel_id=1, source_target_pairs={{0,8},{4,24},{8,0},{12,16},{16,12},{20,28},{24,4},{28,20},{1,9},{5... | collective-permute-start | bytes 580616 | tf_op jit(solution)/shard_map/ppermute | solution.py:165
  368.5 18.1 %collective-permute-start.18 = (f32[2,48,504]{2,1,0:T(8,128)S(1)}, f32[2,48,504]{2,1,0:T(8,128)S(1)}, u32[]{:S(2)}, u32[]{:S(2)}) collective-permute-start(f32[2,48,504]{2,1,0:T(8,128)S(1)} %get-tuple-element.8), channel_id=1, source_target_pairs={{0,0},{4,16},{8,8},{12,24},{16,4},{20,20},{24,12},{28,28},{1,1},{5... | collective-permute-start | bytes 580616 | tf_op jit(solution)/shard_map/ppermute | solution.py:164
  (34 other events, 211.0 us)
